TPU v7x, 32 devices: a whole 2x2x4 slice. The times are simulated.
32 devices in a mesh: rows: 4 (over y, x), cols: 2 (over core), slabs: 4 (over z).
Axes of the slice: x: 2, y: 2, z: 4, core: 2. Of those that a mesh axis runs over, the one named last changes fastest.
Arguments:
- field_values: float32 [16, 64, 512, 128], P('rows', 'cols', 'slabs'), may hold values from 0.5 to 2
- mobility: float32 [16, 64, 512, 128], P('rows', 'cols', 'slabs'), may hold values from 0.03 to 0.15
- source: float32 [16, 64, 512, 128], P('rows', 'cols', 'slabs'), may hold values from -0.2 to 0.2
Outputs:
- anomaly: float32 [16, 64, 512, 128], P('rows', 'cols', 'slabs')
- field_values_end: float32 [16, 64, 512, 128], P('rows', 'cols', 'slabs')
All inputs are finite; a program needn't handle non-finite values.
Results may differ from a plain program's by a relative error of at most 0.00002.
Values sent between devices are 32-bit elements; how exact they have to be, the bound alone decides.
A program may use at most 128 MiB of HBM per device.

v0:
```python
import functools

import jax
import jax.numpy as jnp
from jax import lax
from jax.experimental import pallas as pl
from jax.experimental.pallas import tpu as pltpu
from jax.sharding import PartitionSpec as P

STEPS = 3
MESH = pl.DeviceIdType.MESH


def steps_kernel(
    sizes, spans, f, m, s, out, lines,
    field, mob, src, z_in, z_out, stats, stats_in, tail, tail_in,
    y_send, y_recv, x_send, x_recv, z_send, z_recv, s_send, s_recv, e_send, e_recv, load_sem,
):
    planes, width, depth, _ = f.shape
    rows, cols, slabs = sizes
    chunks = len(spans)
    last = planes - 1
    short = spans[-1][1]

    def shifted(axis, by):
        count = lax.axis_size(axis)
        return {axis: lax.rem(lax.axis_index(axis) + by + count, count)}

    peers = [(axis, 1) for axis in ("rows", "cols")]
    peers += [(axis, -1) for axis, n in (("rows", rows), ("cols", cols)) if n > 2]
    peers += [("slabs", by) for by in range(1, slabs)]
    barrier = pltpu.get_barrier_semaphore()
    for axis, by in peers:
        pl.semaphore_signal(barrier, inc=1, device_id=shifted(axis, by), device_id_type=MESH)
    pl.semaphore_wait(barrier, len(peers))

    def remote(source, target, send, recv, device):
        return pltpu.make_async_remote_copy(
            src_ref=source, dst_ref=target, send_sem=send, recv_sem=recv,
            device_id=device, device_id_type=MESH,
        )

    def y_copy(t, side, k):
        plane = last if side == 0 else 0
        first, count = spans[k]
        span = pl.ds(1 + first, count)
        source = f.at[plane, pl.ds(first, count)] if t == 0 else field.at[t % 2, plane + 1, span]
        target = field.at[t % 2, 0 if side == 0 else planes + 1, span]
        return remote(source, target, y_send.at[t, side, k], y_recv.at[t, side, k],
                      shifted("rows", 1 if side == 0 else -1))

    def x_copy(t, side, p):
        x = width - 1 if side == 0 else 0
        source = f.at[p, x] if t == 0 else field.at[t % 2, p + 1, x + 1]
        target = field.at[t % 2, p + 1, 0 if side == 0 else width + 1]
        return remote(source, target, x_send.at[t, side, p], x_recv.at[t, side, p],
                      shifted("cols", 1 if side == 0 else -1))

    def z_copy(t, side, p):
        return remote(z_out.at[t, side, p], z_in.at[t, side, p],
                      z_send.at[t, side, p], z_recv.at[t, side, p],
                      shifted("slabs", 1 if side == 0 else -1))

    def s_copy(by, p):
        return remote(stats.at[p], stats_in.at[by - 1, p],
                      s_send.at[by - 1, p], s_recv.at[by - 1, p], shifted("slabs", by))

    def e_copy(by):
        return remote(tail, tail_in.at[by - 1], e_send.at[by - 1], e_recv.at[by - 1],
                      shifted("slabs", by))

    def load(array, p):
        inside = pl.ds(1, width)
        if array == 0:
            return pltpu.make_async_copy(f.at[p], field.at[0, p + 1, inside], load_sem.at[0, p])
        if array == 1:
            return pltpu.make_async_copy(m.at[p], mob.at[p], load_sem.at[1, p])
        return pltpu.make_async_copy(s.at[p], src.at[p], load_sem.at[2, p])

    for k in range(chunks):
        for side in (0, 1):
            y_copy(0, side, k).start()
    for array in range(3):
        for p in range(planes):
            load(array, p).start()
    for p in range(planes):
        for side in (0, 1):
            x_copy(0, side, p).start()

    for p in range(planes):
        load(0, p).wait()

        def edge(x, _):
            z_out[0, 0, p, pl.ds(x, 1)] = field[0, p + 1, x + 1, depth - 1:depth]
            z_out[0, 1, p, pl.ds(x, 1)] = field[0, p + 1, x + 1, 0:1]
            return 0

        lax.fori_loop(0, width, edge, 0)
        for side in (0, 1):
            z_copy(0, side, p).start()
    for array in (1, 2):
        for p in range(planes):
            load(array, p).wait()

    def compute(t, p, first, count, ends=False):
        now, after = t % 2, (t + 1) % 2

        def row(x, _):
            c = field[now, p + 1, x + 1]
            level = lax.broadcasted_iota(jnp.int32, c.shape, 0)
            low = jnp.where(level == 0, z_in[t, 0, p, pl.ds(x, 1)], pltpu.roll(c, 1, 0))
            high = jnp.where(level == depth - 1, z_in[t, 1, p, pl.ds(x, 1)],
                             pltpu.roll(c, depth - 1, 0))
            spread = (field[now, p, x + 1] + field[now, p + 2, x + 1]
                      + field[now, p + 1, x] + field[now, p + 1, x + 2] + low + high - 6.0 * c)
            new = c + mob[p, x] * spread + src[p, x]
            if t + 1 < STEPS:
                field[after, p + 1, x + 1] = new
                z_out[t + 1, 0, p, pl.ds(x, 1)] = new[depth - 1:depth]
                z_out[t + 1, 1, p, pl.ds(x, 1)] = new[0:1]
            else:
                out[p, x] = new
                mean = jnp.sum(new, axis=0, keepdims=True) * (1.0 / depth)
                moved = new - mean
                squares = jnp.sum(moved * moved, axis=0, keepdims=True)
                if ends:
                    tail[0 if p == 0 else 1, 0, pl.ds(x - first, 1)] = mean
                    tail[0 if p == 0 else 1, 1, pl.ds(x - first, 1)] = squares
                else:
                    stats[p, 0, pl.ds(x, 1)] = mean
                    stats[p, 1, pl.ds(x, 1)] = squares
            return 0

        lax.fori_loop(first, first + count, row, 0)

    def ready(t, p):
        for side in (0, 1):
            x_copy(t, side, p).wait_recv()
            z_copy(t, side, p).wait_recv()
            if t >= 1:
                x_copy(t - 1, side, p).wait_send()

    def finish(t, p):
        if t + 1 < STEPS:
            for side in (0, 1):
                x_copy(t + 1, side, p).start()
                z_copy(t + 1, side, p).start()
        else:
            for by in range(1, slabs):
                s_copy(by, p).start()

    def combined(own, others):
        total = own[0]
        for other in others:
            total = total + other[0]
        mean = total * (1.0 / slabs)
        away = own[0] - mean
        squares, between = own[1], away * away
        for other in others:
            away = other[0] - mean
            squares, between = squares + other[1], between + away * away
        variance = (squares + depth * between) * (1.0 / (depth * slabs))
        return mean, lax.rsqrt(variance + 0.0001)

    def settle(p):
        for by in range(1, slabs):
            s_copy(by, p).wait_recv()
        lines[p, 0], lines[p, 1] = combined(
            (stats[p, 0], stats[p, 1]),
            [(stats_in[i, p, 0], stats_in[i, p, 1]) for i in range(slabs - 1)])

    for p in (0, last):
        stats[p] = jnp.zeros_like(stats[p])
    for t in range(STEPS):
        for p in range(1, last):
            ready(t, p)
            compute(t, p, 0, width)
            finish(t, p)
        ready(t, 0)
        ready(t, last)
        for k in range(chunks):
            ends = t + 1 == STEPS and k + 1 == chunks
            if ends:
                finish(t, 0)
                finish(t, last)
                for p in range(1, last):
                    settle(p)
            for side in (0, 1):
                p = 0 if side == 0 else last
                y_copy(t, side, k).wait_recv()
                if t >= 1:
                    y_copy(t - 1, 1 - side, k).wait_send()
                compute(t, p, spans[k][0], spans[k][1], ends)
                if t + 1 < STEPS:
                    y_copy(t + 1, 1 - side, k).start()
        if t + 1 < STEPS:
            finish(t, 0)
            finish(t, last)

    for by in range(1, slabs):
        e_copy(by).start()
    settle(0)
    settle(last)
    for by in range(1, slabs):
        e_copy(by).wait_recv()
    for side, p in ((0, 0), (1, last)):
        mean, scale = combined(
            (tail[side, 0], tail[side, 1]),
            [(tail_in[i, side, 0], tail_in[i, side, 1]) for i in range(slabs - 1)])
        lines[p, 0, width - short:width] = mean
        lines[p, 1, width - short:width] = scale

    for side in (0, 1):
        for k in range(chunks):
            y_copy(STEPS - 1, side, k).wait_send()
        for p in range(planes):
            x_copy(STEPS - 1, side, p).wait_send()
            for t in range(STEPS):
                z_copy(t, side, p).wait_send()
    for p in range(planes):
        for by in range(1, slabs):
            s_copy(by, p).wait_send()
    for by in range(1, slabs):
        e_copy(by).wait_send()


def scale_kernel(
    part, block, line, anomaly, out, scaled, out_sem, anomaly_sem
):
    planes, width = block.shape[:2]
    pieces = [(p, first) for p in range(planes) for first in range(0, width, part)]

    def copy(source, target, sems, i):
        p, first = pieces[i]
        at = (p, pl.ds(first, part))
        return pltpu.make_async_copy(source.at[at], target.at[at], sems.at[i])

    for i in range(len(pieces)):
        copy(block, out, out_sem, i).start()
    for i, (p, first) in enumerate(pieces):

        def row(x, _):
            centred = block[p, x] - line[p, 0, pl.ds(x, 1)]
            scaled[p, x] = centred * line[p, 1, pl.ds(x, 1)]
            return 0

        lax.fori_loop(first, first + part, row, 0)
        copy(scaled, anomaly, anomaly_sem, i).start()
    for i in range(len(pieces)):
        copy(block, out, out_sem, i).wait()
        copy(scaled, anomaly, anomaly_sem, i).wait()


def spans_of(width):
    size, first, spans = max(width // 4, 1), 0, []
    while first < width:
        if width - first <= size:
            size = max((width - first) // 2, min(2, width - first))
        spans.append((first, size))
        first += size
    return tuple(spans)


def per_device(sizes, field_values, mobility, source):
    planes, width, depth, levels = field_values.shape
    slabs = sizes[2]
    spans = spans_of(width)
    chunks, short = len(spans), spans[-1][1]
    f32 = jnp.float32
    dma = pltpu.SemaphoreType.DMA
    any_space = pl.BlockSpec(memory_space=pl.ANY)
    held = pl.BlockSpec(memory_space=pltpu.VMEM)
    line = (planes, 2, width, levels)
    whole = jax.ShapeDtypeStruct(field_values.shape, f32)
    end, lines = pl.pallas_call(
        functools.partial(steps_kernel, sizes, spans),
        out_shape=(pltpu.VMEM(field_values.shape, f32), pltpu.VMEM(line, f32)),
        in_specs=[any_space] * 3,
        out_specs=(held, held),
        scratch_shapes=[
            pltpu.VMEM((2, planes + 2, width + 2, depth, levels), f32),
            pltpu.VMEM(field_values.shape, f32),
            pltpu.VMEM(field_values.shape, f32),
            pltpu.VMEM((STEPS, 2, planes, width, levels), f32),
            pltpu.VMEM((STEPS, 2, planes, width, levels), f32),
            pltpu.VMEM(line, f32),
            pltpu.VMEM((slabs - 1,) + line, f32),
            pltpu.VMEM((2, 2, short, levels), f32),
            pltpu.VMEM((slabs - 1, 2, 2, short, levels), f32),
            dma((STEPS, 2, chunks)), dma((STEPS, 2, chunks)),
            dma((STEPS, 2, planes)), dma((STEPS, 2, planes)),
            dma((STEPS, 2, planes)), dma((STEPS, 2, planes)),
            dma((slabs - 1, planes)), dma((slabs - 1, planes)),
            dma((slabs - 1,)), dma((slabs - 1,)),
            dma((3, planes)),
        ],
        compiler_params=pltpu.CompilerParams(
            collective_id=0, has_side_effects=True, vmem_limit_bytes=46 * 1024 * 1024),
    )(field_values, mobility, source)

    part = max(width // 4, 1)
    pieces = planes * (width // part)
    return pl.pallas_call(
        functools.partial(scale_kernel, part),
        out_shape=(whole, whole),
        in_specs=[held, held],
        out_specs=(any_space, any_space),
        scratch_shapes=[
            pltpu.VMEM(field_values.shape, f32),
            dma((pieces,)), dma((pieces,)),
        ],
        compiler_params=pltpu.CompilerParams(vmem_limit_bytes=20 * 1024 * 1024),
    )(end, lines)


def solution(mesh):
    sizes = tuple(mesh.shape[axis] for axis in ("rows", "cols", "slabs"))
    spec = P("rows", "cols", "slabs", None)
    return jax.shard_map(
        functools.partial(per_device, sizes),
        mesh=mesh,
        in_specs=(spec, spec, spec),
        out_specs=(spec, spec),
        check_vma=False,
    )
```

profile of v0, /device:TPU:1, one launch (start us, length us, event | category | flops | bytes accessed | tf_op | source)
XLA Modules:
  0.0 287.4 jit_solution(5423779504648041253)
XLA Ops:
  0.6 280.7 %shard_map.50 = (f32[4,32,128,128]{3,2,1,0:T(8,128)S(1)}, f32[4,2,32,128]{3,2,1,0:T(8,128)S(1)}) custom-call(f32[4,32,128,128]{3,2,1,0:T(8,128)} %f.1, f32[4,32,128,128]{3,2,1,0:T(8,128)} %m.1, f32[4,32,128,128]{3,2,1,0:T(8,128)} %s.1), custom_call_target="tpu_custom_call" | custom-call | tf_op jit(solution)/shard_map/pallas_call | solution.py:275
  281.3 6.1 %shard_map.51 = (f32[4,32,128,128]{3,2,1,0:T(8,128)}, f32[4,32,128,128]{3,2,1,0:T(8,128)}) custom-call(f32[4,32,128,128]{3,2,1,0:T(8,128)S(1)} %get-tuple-element.4.block, f32[4,2,32,128]{3,2,1,0:T(8,128)S(1)} %get-tuple-element.5.line), custom_call_target="tpu_custom_call" | custom-call | tf_op jit(solution)/shard_map/pallas_call | solution.py:303
where the time goes:
time: 290 us; the launch traced here: 287 us
  Pallas kernels  287 us (99%)
    pallas_call x1, Pallas kernels, per_device(): pl.pallas_call(functools.partial(steps_kernel, sizes, spans), out_shape=(...  281 us
    pallas_call x1, Pallas kernels, per_device(): pl.pallas_call(functools.partial(scale_kernel, part), out_shape=(whole, w...  6.08 us

commit v1 on v0

--- a/solution.py
+++ b/solution.py
@@ -14,7 +14,7 @@
 def steps_kernel(
     sizes, spans, f, m, s, out, lines,
     field, mob, src, z_in, z_out, stats, stats_in, tail, tail_in,
-    y_send, y_recv, x_send, x_recv, z_send, z_recv, s_send, s_recv, e_send, e_recv, load_sem,
+    y_send, y_recv, w_send, w_recv, x_send, x_recv, z_send, z_recv, s_send, s_recv, e_send, e_recv, load_sem,
 ):
     planes, width, depth, _ = f.shape
     rows, cols, slabs = sizes
@@ -32,6 +32,29 @@
     barrier = pltpu.get_barrier_semaphore()
     for axis, by in peers:
         pl.semaphore_signal(barrier, inc=1, device_id=shifted(axis, by), device_id_type=MESH)
+    ends = (0, last)
+    early = spans[0][1]
+
+    def load(array, p, part=0):
+        if array == 0:
+            first, count = (0, early) if part == 0 else (early, width - early)
+            return pltpu.make_async_copy(
+                f.at[p, pl.ds(first, count)], field.at[0, p + 1, pl.ds(1 + first, count)],
+                load_sem.at[3 * part, p])
+        if array == 1:
+            return pltpu.make_async_copy(m.at[p], mob.at[p], load_sem.at[1, p])
+        return pltpu.make_async_copy(s.at[p], src.at[p], load_sem.at[2, p])
+
+    inner = tuple(range(1, last))
+    for part in (0, 1):
+        for p in ends:
+            load(0, p, part).start()
+    for p in inner:
+        for part in (0, 1):
+            load(0, p, part).start()
+    for array in (1, 2):
+        for p in range(planes):
+            load(array, p).start()
     pl.semaphore_wait(barrier, len(peers))
 
     def remote(source, target, send, recv, device):
@@ -40,18 +63,19 @@
             device_id=device, device_id_type=MESH,
         )
 
-    def y_copy(t, side, k):
-        plane = last if side == 0 else 0
+    def y_copy(t, side, k, less=0):
+        plane = last * (1 - side)
         first, count = spans[k]
+        count -= less
         span = pl.ds(1 + first, count)
-        source = f.at[plane, pl.ds(first, count)] if t == 0 else field.at[t % 2, plane + 1, span]
-        target = field.at[t % 2, 0 if side == 0 else planes + 1, span]
+        source = field.at[t % 2, plane + 1, span]
+        target = field.at[t % 2, (planes + 1) * side, span]
         return remote(source, target, y_send.at[t, side, k], y_recv.at[t, side, k],
-                      shifted("rows", 1 if side == 0 else -1))
+                      shifted("rows", 1 - 2 * side))
 
     def x_copy(t, side, p):
         x = width - 1 if side == 0 else 0
-        source = f.at[p, x] if t == 0 else field.at[t % 2, p + 1, x + 1]
+        source = field.at[t % 2, p + 1, x + 1]
         target = field.at[t % 2, p + 1, 0 if side == 0 else width + 1]
         return remote(source, target, x_send.at[t, side, p], x_recv.at[t, side, p],
                       shifted("cols", 1 if side == 0 else -1))
@@ -69,26 +93,53 @@
         return remote(tail, tail_in.at[by - 1], e_send.at[by - 1], e_recv.at[by - 1],
                       shifted("slabs", by))
 
-    def load(array, p):
-        inside = pl.ds(1, width)
-        if array == 0:
-            return pltpu.make_async_copy(f.at[p], field.at[0, p + 1, inside], load_sem.at[0, p])
-        if array == 1:
-            return pltpu.make_async_copy(m.at[p], mob.at[p], load_sem.at[1, p])
-        return pltpu.make_async_copy(s.at[p], src.at[p], load_sem.at[2, p])
-
-    for k in range(chunks):
-        for side in (0, 1):
-            y_copy(0, side, k).start()
-    for array in range(3):
-        for p in range(planes):
-            load(array, p).start()
-    for p in range(planes):
+    odd = lax.rem(lax.axis_index("rows"), 2)
+    sides = [lax.rem(odd + i, 2) for i in range(2)]
+    second = lax.rem(lax.axis_index("cols"), 2) == 1
+    forward = cols % 2 == 0 and spans[-1][1] > 1
+
+    def w_copy(side):
+        plane = last * (1 - side)
+        return remote(field.at[0, plane + 1, 0], field.at[0, (planes + 1) * side, width],
+                      w_send.at[side], w_recv.at[side],
+                      {"rows": shifted("rows", 1 - 2 * side)["rows"],
+                       "cols": shifted("cols", -1)["cols"]})
+
+    def on_last(act):
+        if not forward:
+            act(0, False)
+            return
+        pl.when(second)(lambda: act(0, False))
+        pl.when(jnp.logical_not(second))(lambda: act(1, True))
+
+    for part in (0, 1):
+        for p in ends:
+            load(0, p, part).wait()
+        for k in ((0,), range(1, chunks - 1))[part]:
+            for side in sides:
+                y_copy(0, 1 - side, k).start()
+    for p in ends + inner:
+        if p in inner:
+            for part in (0, 1):
+                load(0, p, part).wait()
         for side in (0, 1):
             x_copy(0, side, p).start()
 
+    for p in ends:
+        x_copy(0, 0, p).wait_recv()
+
+    def send_last(less, _):
+        for side in sides:
+            y_copy(0, 1 - side, chunks - 1, less).start()
+
+    if forward:
+        @pl.when(second)
+        def _():
+            for side in sides:
+                w_copy(1 - side).start()
+    on_last(send_last)
+
     for p in range(planes):
-        load(0, p).wait()
 
         def edge(x, _):
             z_out[0, 0, p, pl.ds(x, 1)] = field[0, p + 1, x + 1, depth - 1:depth]
@@ -102,7 +153,7 @@
         for p in range(planes):
             load(array, p).wait()
 
-    def compute(t, p, first, count, ends=False):
+    def compute(t, p, first, count, at=None):
         now, after = t % 2, (t + 1) % 2
 
         def row(x, _):
@@ -123,9 +174,9 @@
                 mean = jnp.sum(new, axis=0, keepdims=True) * (1.0 / depth)
                 moved = new - mean
                 squares = jnp.sum(moved * moved, axis=0, keepdims=True)
-                if ends:
-                    tail[0 if p == 0 else 1, 0, pl.ds(x - first, 1)] = mean
-                    tail[0 if p == 0 else 1, 1, pl.ds(x - first, 1)] = squares
+                if at is not None:
+                    tail[at, 0, pl.ds(x - first, 1)] = mean
+                    tail[at, 1, pl.ds(x - first, 1)] = squares
                 else:
                     stats[p, 0, pl.ds(x, 1)] = mean
                     stats[p, 1, pl.ds(x, 1)] = squares
@@ -135,7 +186,8 @@
 
     def ready(t, p):
         for side in (0, 1):
-            x_copy(t, side, p).wait_recv()
+            if t or side or p not in ends:
+                x_copy(t, side, p).wait_recv()
             z_copy(t, side, p).wait_recv()
             if t >= 1:
                 x_copy(t - 1, side, p).wait_send()
@@ -179,20 +231,42 @@
         ready(t, 0)
         ready(t, last)
         for k in range(chunks):
-            ends = t + 1 == STEPS and k + 1 == chunks
-            if ends:
+            tailed = t + 1 == STEPS and k + 1 == chunks
+            if tailed:
                 finish(t, 0)
                 finish(t, last)
                 for p in range(1, last):
                     settle(p)
-            for side in (0, 1):
-                p = 0 if side == 0 else last
-                y_copy(t, side, k).wait_recv()
-                if t >= 1:
+            for side in sides:
+                p = side * last
+                if t == 0 and k + 1 == chunks:
+
+                    def arrive(less, passed, side=side):
+                        y_copy(0, side, chunks - 1, less).wait_recv()
+                        if passed:
+                            w_copy(side).wait_recv()
+
+                    on_last(arrive)
+                else:
+                    y_copy(t, side, k).wait_recv()
+                if t == 1 and k + 1 == chunks:
+
+                    def left(less, _, side=side):
+                        y_copy(0, 1 - side, chunks - 1, less).wait_send()
+
+                    on_last(left)
+                elif t >= 1:
                     y_copy(t - 1, 1 - side, k).wait_send()
-                compute(t, p, spans[k][0], spans[k][1], ends)
+                compute(t, p, spans[k][0], spans[k][1], side if tailed else None)
                 if t + 1 < STEPS:
                     y_copy(t + 1, 1 - side, k).start()
+        if t == 0 and forward:
+
+            @pl.when(second)
+            def _():
+                for side in (0, 1):
+                    w_copy(side).wait_send()
+
         if t + 1 < STEPS:
             finish(t, 0)
             finish(t, last)
@@ -288,11 +362,12 @@
             pltpu.VMEM((2, 2, short, levels), f32),
             pltpu.VMEM((slabs - 1, 2, 2, short, levels), f32),
             dma((STEPS, 2, chunks)), dma((STEPS, 2, chunks)),
+            dma((2,)), dma((2,)),
             dma((STEPS, 2, planes)), dma((STEPS, 2, planes)),
             dma((STEPS, 2, planes)), dma((STEPS, 2, planes)),
             dma((slabs - 1, planes)), dma((slabs - 1, planes)),
             dma((slabs - 1,)), dma((slabs - 1,)),
-            dma((3, planes)),
+            dma((4, planes)),
         ],
         compiler_params=pltpu.CompilerParams(
             collective_id=0, has_side_effects=True, vmem_limit_bytes=46 * 1024 * 1024),

time: 290 us -> 287 us (0.990)
  no operation moved by 1% of the time
where the time goes in v1:
time: 287 us
  Pallas kernels  287 us (100%)
    pallas_call x1, Pallas kernels, per_device(): pl.pallas_call(functools.partial(steps_kernel, sizes, spans), out_shape=(...  280 us
    pallas_call x1, Pallas kernels, per_device(): pl.pallas_call(functools.partial(scale_kernel, part), out_shape=(whole, w...  6.08 us

profile of v1, /device:TPU:1, one launch (start us, length us, event | category | flops | bytes accessed | tf_op | source)
XLA Modules:
  0.0 287.2 jit_solution(7754059500112029707)
XLA Ops:
  0.6 280.4 %shard_map.50 = (f32[4,32,128,128]{3,2,1,0:T(8,128)S(1)}, f32[4,2,32,128]{3,2,1,0:T(8,128)S(1)}) custom-call(f32[4,32,128,128]{3,2,1,0:T(8,128)} %f.1, f32[4,32,128,128]{3,2,1,0:T(8,128)} %m.1, f32[4,32,128,128]{3,2,1,0:T(8,128)} %s.1), custom_call_target="tpu_custom_call" | custom-call | tf_op jit(solution)/shard_map/pallas_call | solution.py:349
  281.1 6.1 %shard_map.51 = (f32[4,32,128,128]{3,2,1,0:T(8,128)}, f32[4,32,128,128]{3,2,1,0:T(8,128)}) custom-call(f32[4,32,128,128]{3,2,1,0:T(8,128)S(1)} %get-tuple-element.4.block, f32[4,2,32,128]{3,2,1,0:T(8,128)S(1)} %get-tuple-element.5.line), custom_call_target="tpu_custom_call" | custom-call | tf_op jit(solution)/shard_map/pallas_call | solution.py:378

commit v2 on v1

--- a/solution.py
+++ b/solution.py
@@ -93,8 +93,8 @@
         return remote(tail, tail_in.at[by - 1], e_send.at[by - 1], e_recv.at[by - 1],
                       shifted("slabs", by))
 
-    odd = lax.rem(lax.axis_index("rows"), 2)
-    sides = [lax.rem(odd + i, 2) for i in range(2)]
+    wraps = (lax.rem(lax.axis_index("rows") + 1, rows) < 2).astype(jnp.int32)
+    sides = [lax.rem(wraps + i, 2) for i in range(2)]
     second = lax.rem(lax.axis_index("cols"), 2) == 1
     forward = cols % 2 == 0 and spans[-1][1] > 1
 

time: 287 us -> 287 us (level)
  no operation moved by 1% of the time
where the time goes in v2:
time: 287 us
  Pallas kernels  286 us (100%)
    pallas_call x1, Pallas kernels, per_device(): pl.pallas_call(functools.partial(steps_kernel, sizes, spans), out_shape=(...  280 us
    pallas_call x1, Pallas kernels, per_device(): pl.pallas_call(functools.partial(scale_kernel, part), out_shape=(whole, w...  6.08 us

profile of v2, /device:TPU:1, one launch (start us, length us, event | category | flops | bytes accessed | tf_op | source)
XLA Modules:
  0.0 286.7 jit_solution(18014305419782990125)
XLA Ops:
  0.6 280.0 %shard_map.50 = (f32[4,32,128,128]{3,2,1,0:T(8,128)S(1)}, f32[4,2,32,128]{3,2,1,0:T(8,128)S(1)}) custom-call(f32[4,32,128,128]{3,2,1,0:T(8,128)} %f.1, f32[4,32,128,128]{3,2,1,0:T(8,128)} %m.1, f32[4,32,128,128]{3,2,1,0:T(8,128)} %s.1), custom_call_target="tpu_custom_call" | custom-call | tf_op jit(solution)/shard_map/pallas_call | solution.py:349
  280.6 6.1 %shard_map.51 = (f32[4,32,128,128]{3,2,1,0:T(8,128)}, f32[4,32,128,128]{3,2,1,0:T(8,128)}) custom-call(f32[4,32,128,128]{3,2,1,0:T(8,128)S(1)} %get-tuple-element.4.block, f32[4,2,32,128]{3,2,1,0:T(8,128)S(1)} %get-tuple-element.5.line), custom_call_target="tpu_custom_call" | custom-call | tf_op jit(solution)/shard_map/pallas_call | solution.py:378

commit v3 on v2

--- a/solution.py
+++ b/solution.py
@@ -46,15 +46,8 @@
         return pltpu.make_async_copy(s.at[p], src.at[p], load_sem.at[2, p])
 
     inner = tuple(range(1, last))
-    for part in (0, 1):
-        for p in ends:
-            load(0, p, part).start()
-    for p in inner:
-        for part in (0, 1):
-            load(0, p, part).start()
-    for array in (1, 2):
-        for p in range(planes):
-            load(array, p).start()
+    for p in ends:
+        load(0, p).start()
     pl.semaphore_wait(barrier, len(peers))
 
     def remote(source, target, send, recv, device):
@@ -118,6 +111,12 @@
         for k in ((0,), range(1, chunks - 1))[part]:
             for side in sides:
                 y_copy(0, 1 - side, k).start()
+        if part == 0:
+            for p in ends:
+                load(0, p, 1).start()
+            for p in inner:
+                for late in (0, 1):
+                    load(0, p, late).start()
     for p in ends + inner:
         if p in inner:
             for part in (0, 1):
@@ -149,8 +148,9 @@
         lax.fori_loop(0, width, edge, 0)
         for side in (0, 1):
             z_copy(0, side, p).start()
-    for array in (1, 2):
-        for p in range(planes):
+    for p in inner + ends:
+        for array in (1, 2):
+            load(array, p).start()
             load(array, p).wait()
 
     def compute(t, p, first, count, at=None):
@@ -326,13 +326,14 @@
 
 
 def spans_of(width):
-    size, first, spans = max(width // 4, 1), 0, []
-    while first < width:
-        if width - first <= size:
-            size = max((width - first) // 2, min(2, width - first))
-        spans.append((first, size))
+    short = min(2, width)
+    first, spans = 0, []
+    for i in range(3):
+        size = (width - short - first) // (3 - i)
+        if size:
+            spans.append((first, size))
         first += size
-    return tuple(spans)
+    return tuple(spans) + ((first, width - first),)
 
 
 def per_device(sizes, field_values, mobility, source):

time: 287 us -> 287 us (level)
  no operation moved by 1% of the time
where the time goes in v3:
time: 287 us
  Pallas kernels  286 us (100%)
    pallas_call x1, Pallas kernels, per_device(): pl.pallas_call(functools.partial(steps_kernel, sizes, spans), out_shape=(...  280 us
    pallas_call x1, Pallas kernels, per_device(): pl.pallas_call(functools.partial(scale_kernel, part), out_shape=(whole, w...  6.08 us

profile of v3, /device:TPU:1, one launch (start us, length us, event | category | flops | bytes accessed | tf_op | source)
XLA Modules:
  0.0 286.9 jit_solution(8622904290571891215)
XLA Ops:
  0.6 280.1 %shard_map.50 = (f32[4,32,128,128]{3,2,1,0:T(8,128)S(1)}, f32[4,2,32,128]{3,2,1,0:T(8,128)S(1)}) custom-call(f32[4,32,128,128]{3,2,1,0:T(8,128)} %f.1, f32[4,32,128,128]{3,2,1,0:T(8,128)} %m.1, f32[4,32,128,128]{3,2,1,0:T(8,128)} %s.1), custom_call_target="tpu_custom_call" | custom-call | tf_op jit(solution)/shard_map/pallas_call | solution.py:350
  280.8 6.1 %shard_map.51 = (f32[4,32,128,128]{3,2,1,0:T(8,128)}, f32[4,32,128,128]{3,2,1,0:T(8,128)}) custom-call(f32[4,32,128,128]{3,2,1,0:T(8,128)S(1)} %get-tuple-element.4.block, f32[4,2,32,128]{3,2,1,0:T(8,128)S(1)} %get-tuple-element.5.line), custom_call_target="tpu_custom_call" | custom-call | tf_op jit(solution)/shard_map/pallas_call | solution.py:379
